TPU v7x, 32 devices: a whole 2x2x4 slice. The times are simulated.
32 devices in a mesh: dom: 8 (over z, x), sub: 4 (over y, core).
Axes of the slice: x: 2, y: 2, z: 4, core: 2. Of those that a mesh axis runs over, the one named last changes fastest.
Arguments:
- level_set: float32 [64, 32, 128], P('dom', 'sub'), may hold values from 0 to 1
- velocity: float32 [3, 64, 32, 128], P(None, 'dom', 'sub'), may hold values from -6 to 6
- source: float32 [64, 32, 128], P('dom', 'sub'), may hold values from -12 to 12
Outputs:
- new_level: float32 [64, 32, 128], P('dom', 'sub')
- pressure: float32 [64, 32, 128], P('dom', 'sub')
- correction: float32 [64, 32, 128], P('dom', 'sub')
All inputs are finite; a program needn't handle non-finite values.
Results may differ from a plain program's by a relative error of at most 0.0003.
Values sent between devices are 32-bit elements; how exact they have to be, the bound alone decides.
A program may use at most 64 MiB of HBM per device.

v0:
```python
import math

import jax
import jax.numpy as jnp
import numpy as np
from jax import lax
from jax.sharding import PartitionSpec as P

SWEEPS = 2
PITERS = 2


gll_nodes = [
    -1.0,
    -0.8717401485096066,
    -0.5917001814331423,
    -0.2092992179024789,
    0.2092992179024789,
    0.5917001814331423,
    0.8717401485096066,
    1.0,
]
advect_step = 0.05
reinit_step = 0.02
interface_width = 0.1
density_ratio = 9.0


def padded(x, sides, width):
    for axis, dim in sides:
        devices, length = (lax.axis_size(axis), x.shape[dim])
        up = [(i, (i + 1) % devices) for i in range(devices)]
        down = [(j, i) for i, j in up]
        last = lax.slice_in_dim(x, length - width, length, axis=dim)
        leading = lax.slice_in_dim(x, 0, width, axis=dim)
        before = lax.ppermute(last, axis, up)
        after = lax.ppermute(leading, axis, down)
        x = jnp.concatenate([before, x, after], axis=dim)
    return x


def tables():
    node_points = np.array(gll_nodes)
    poly_order = 7
    values_prev = np.ones(8)
    values_now = node_points.copy()
    for degree in range(1, poly_order):
        values_next = ((2 * degree + 1) * node_points * values_now - degree * values_prev) / (
            degree + 1
        )
        values_prev, values_now = (values_now, values_next)
    matrix = np.zeros((8, 8))
    for line in range(8):
        for column in range(8):
            if line != column:
                matrix[line, column] = values_now[line] / (
                    values_now[column] * (node_points[line] - node_points[column])
                )
    matrix[0, 0] = -poly_order * (poly_order + 1) / 4.0
    matrix[7, 7] = poly_order * (poly_order + 1) / 4.0
    weights = 2.0 / (poly_order * (poly_order + 1) * values_now**2)
    return (matrix, weights)


def point_tables(full_shape, weights):
    corner_count = np.array([2.0, 1.0, 1.0, 1.0, 1.0, 1.0, 1.0, 2.0])
    weight_lines = []
    count_lines = []
    for dim_index in (1, 2, 3):
        repeats = full_shape[dim_index] // 8
        weight_lines.append(jnp.asarray(np.tile(weights, repeats), jnp.float32))
        count_lines.append(jnp.asarray(np.tile(1.0 / corner_count, repeats), jnp.float32))
    weight_cube = (
        weight_lines[0][:, None, None]
        * weight_lines[1][None, :, None]
        * weight_lines[2][None, None, :]
    )[None]
    inv_mult = (
        count_lines[0][:, None, None]
        * count_lines[1][None, :, None]
        * count_lines[2][None, None, :]
    )[None]
    return (weight_cube, inv_mult)


def derive(values, dim_index, matrix):
    full_shape = values.shape
    highest = lax.Precision.HIGHEST
    if dim_index == 1:
        blocks = values.reshape((full_shape[0], full_shape[1] // 8, 8) + full_shape[2:])
        result = jnp.einsum(
            "baipq,ji->bajpq", blocks, jnp.asarray(matrix, jnp.float32), precision=highest
        )
    elif dim_index == 2:
        blocks = values.reshape(full_shape[:2] + (full_shape[2] // 8, 8, full_shape[3]))
        result = jnp.einsum(
            "bpaiq,ji->bpajq", blocks, jnp.asarray(matrix, jnp.float32), precision=highest
        )
    else:
        block_width = math.gcd(full_shape[3], 128)
        block_matrix = jnp.asarray(np.kron(np.eye(block_width // 8), matrix), jnp.float32)
        blocks = values.reshape(full_shape[:3] + (full_shape[3] // block_width, block_width))
        result = jnp.einsum("bpqai,ji->bpqaj", blocks, block_matrix, precision=highest)
    return result.reshape(full_shape)


def gradient(values, matrix):
    return [derive(values, 1, matrix), derive(values, 2, matrix), derive(values, 3, matrix)]


def join_edges(values, upper, lower, dim_index):
    position = lax.broadcasted_iota(jnp.int32, values.shape, dim_index) % 8
    return values + jnp.where(position == 7, upper, 0.0) + jnp.where(position == 0, lower, 0.0)


def fold_faces(widened, dim_index, length):
    values = lax.slice_in_dim(widened, 1, length + 1, axis=dim_index)
    upper = lax.slice_in_dim(widened, 2, length + 2, axis=dim_index)
    lower = lax.slice_in_dim(widened, 0, length, axis=dim_index)
    return join_edges(values, upper, lower, dim_index)


def fold_local(values, dim_index):
    upper = jnp.roll(values, -1, axis=dim_index)
    lower = jnp.roll(values, 1, axis=dim_index)
    return join_edges(values, upper, lower, dim_index)


def assemble(values):
    widened = padded(values, (("dom", 1),), 1)
    values = fold_faces(widened, 1, values.shape[1])
    widened = padded(values, (("sub", 2),), 1)
    values = fold_faces(widened, 2, values.shape[2])
    return fold_local(values, 3)


def both_sums(residual, precond, applied, inv_mult):
    return lax.psum(
        (jnp.sum(residual * precond * inv_mult), jnp.sum(precond * applied * inv_mult)),
        ("dom", "sub"),
    )


def local(level_set, velocity, source):
    matrix, weights = tables()
    phase_field = level_set[None]
    weight_cube, inv_mult = point_tables(phase_field.shape, weights)
    gradients = gradient(phase_field, matrix)
    advected = phase_field - advect_step * (
        velocity[0:1] * gradients[0] + velocity[1:2] * gradients[1] + velocity[2:3] * gradients[2]
    )
    phase_field = assemble(advected) * inv_mult
    gradients = gradient(phase_field, matrix)
    magnitude = jnp.sqrt(
        gradients[0] * gradients[0] + gradients[1] * gradients[1] + gradients[2] * gradients[2]
    )
    scaled = 1.0 / jnp.maximum(magnitude, 1.0)
    normals = [gradients[0] * scaled, gradients[1] * scaled, gradients[2] * scaled]
    for sweep_index in range(SWEEPS):
        if sweep_index > 0:
            gradients = gradient(phase_field, matrix)
        compress = phase_field * (1.0 - phase_field)
        change = derive(interface_width * gradients[0] - compress * normals[0], 1, matrix)
        change = change + derive(interface_width * gradients[1] - compress * normals[1], 2, matrix)
        change = change + derive(interface_width * gradients[2] - compress * normals[2], 3, matrix)
        phase_field = phase_field + reinit_step * assemble(change) * inv_mult
    mobility = 1.0 / (1.0 + density_ratio * phase_field * phase_field)
    weighted = weight_cube * mobility
    square_t = (matrix * matrix).T
    diag_local = (
        weight_cube
        + derive(weighted, 1, square_t)
        + derive(weighted, 2, square_t)
        + derive(weighted, 3, square_t)
    )
    assembled = assemble(jnp.concatenate([weight_cube * source[None], diag_local], axis=0))
    right_side = assembled[0:1]
    diagonal = assembled[1:2]
    transposed = matrix.T

    def operate(direction):
        grads_dir = gradient(direction, matrix)
        local_sum = weight_cube * direction + derive(weighted * grads_dir[0], 1, transposed)
        local_sum = (
            local_sum
            + derive(weighted * grads_dir[1], 2, transposed)
            + derive(weighted * grads_dir[2], 3, transposed)
        )
        return assemble(local_sum)

    solution = jnp.zeros_like(right_side)
    residual = right_side
    precond = residual / diagonal
    applied = operate(precond)
    norm_now, product = both_sums(residual, precond, applied, inv_mult)
    step_size = norm_now / product
    direction = precond
    along_image = applied
    for step_index in range(PITERS):
        solution = solution + step_size * direction
        residual = residual - step_size * along_image
        if step_index + 1 < PITERS:
            precond = residual / diagonal
            applied = operate(precond)
            norm_next, product = both_sums(residual, precond, applied, inv_mult)
            ratio_new = norm_next / norm_now
            step_size = norm_next / (product - ratio_new * norm_next / step_size)
            direction = precond + ratio_new * direction
            along_image = applied + ratio_new * along_image
            norm_now = norm_next
    return (phase_field[0], solution[0], (residual / diagonal)[0])


def solution(mesh):
    return jax.shard_map(
        local,
        mesh=mesh,
        in_specs=(P("dom", "sub", None), P(None, "dom", "sub", None), P("dom", "sub", None)),
        out_specs=(P("dom", "sub", None), P("dom", "sub", None), P("dom", "sub", None)),
        check_vma=False,
    )
```

profile of v0, /device:TPU:0, one launch (start us, length us, event | category | flops | bytes accessed | tf_op | source)
XLA Modules:
  0.0 164.9 jit_solution(13758522378719981348)
XLA Ops:
  0.7 0.8 fusion.168
  1.8 0.7 copy-done
  2.7 6.1 %collective-permute-start = (f32[1,1,8,128]{3,1,2,0:T(1,128)S(1)}, f32[1,1,8,128]{3,1,2,0:T(1,128)S(1)}, u32[]{:S(2)}, u32[]{:S(2)}) collective-permute-start(f32[1,1,8,128]{3,1,2,0:T(1,128)S(1)} %get-tuple-element.73), channel_id=1, source_target_pairs={{4,0},{8,4},{12,8},{16,12},{20,16},{24,20},{28,24},{0,28},{5,1},{9... | collective-permute-start | bytes 12296 | tf_op jit(solution)/shard_map/ppermute | solution.py:37
  8.8 0.6 copy-done.10
  9.6 0.6 collective-permute-done
  10.1 5.0 %collective-permute-done.1 = f32[1,1,8,128]{3,1,2,0:T(1,128)S(1)} collective-permute-done((f32[1,1,8,128]{3,1,2,0:T(1,128)S(1)}, f32[1,1,8,128]{3,1,2,0:T(1,128)S(1)}, u32[]{:S(2)}, u32[]{:S(2)}) %collective-permute-start.1) | collective-permute-done | bytes 4128 | tf_op jit(solution)/shard_map/ppermute | solution.py:36
  15.3 0.5 collective-permute-start.3
  15.8 0.8 collective-permute-done.2
  16.6 1.8 %collective-permute-done.3 = f32[1,8,1,128]{3,1,2,0:T(8,128)S(1)} collective-permute-done((f32[1,8,1,128]{3,1,2,0:T(8,128)S(1)}, f32[1,8,1,128]{3,1,2,0:T(8,128)S(1)}, u32[]{:S(2)}, u32[]{:S(2)}) %collective-permute-start.3) | collective-permute-done | bytes 4128 | tf_op jit(solution)/shard_map/ppermute | solution.py:36
  18.6 0.7 copy-done.6
  20.7 2.0 %collective-permute-start.5 = (f32[1,1,8,128]{3,1,2,0:T(1,128)S(1)}, f32[1,1,8,128]{3,1,2,0:T(1,128)S(1)}, u32[]{:S(2)}, u32[]{:S(2)}) collective-permute-start(f32[1,1,8,128]{3,1,2,0:T(1,128)S(1)} %get-tuple-element.62), channel_id=1, source_target_pairs={{0,4},{4,8},{8,12},{12,16},{16,20},{20,24},{24,28},{28,0},{1,5},{5... | collective-permute-start | bytes 12296 | tf_op jit(solution)/shard_map/ppermute | solution.py:36
  22.8 1.6 collective-permute-done.4
  24.3 2.8 %collective-permute-done.5 = f32[1,1,8,128]{3,1,2,0:T(1,128)S(1)} collective-permute-done((f32[1,1,8,128]{3,1,2,0:T(1,128)S(1)}, f32[1,1,8,128]{3,1,2,0:T(1,128)S(1)}, u32[]{:S(2)}, u32[]{:S(2)}) %collective-permute-start.5) | collective-permute-done | bytes 4128 | tf_op jit(solution)/shard_map/ppermute | solution.py:36
  27.3 0.5 collective-permute-start.7
  27.7 0.8 collective-permute-done.6
  28.6 1.8 %collective-permute-done.7 = f32[1,8,1,128]{3,1,2,0:T(8,128)S(1)} collective-permute-done((f32[1,8,1,128]{3,1,2,0:T(8,128)S(1)}, f32[1,8,1,128]{3,1,2,0:T(8,128)S(1)}, u32[]{:S(2)}, u32[]{:S(2)}) %collective-permute-start.7) | collective-permute-done | bytes 4128 | tf_op jit(solution)/shard_map/ppermute | solution.py:36
  32.1 2.0 %collective-permute-start.9 = (f32[1,1,8,128]{3,1,2,0:T(1,128)S(1)}, f32[1,1,8,128]{3,1,2,0:T(1,128)S(1)}, u32[]{:S(2)}, u32[]{:S(2)}) collective-permute-start(f32[1,1,8,128]{3,1,2,0:T(1,128)S(1)} %get-tuple-element.54), channel_id=1, source_target_pairs={{0,4},{4,8},{8,12},{12,16},{16,20},{20,24},{24,28},{28,0},{1,5},{5... | collective-permute-start | bytes 12296 | tf_op jit(solution)/shard_map/ppermute | solution.py:36
  34.1 1.5 collective-permute-done.8
  35.6 2.8 %collective-permute-done.9 = f32[1,1,8,128]{3,1,2,0:T(1,128)S(1)} collective-permute-done((f32[1,1,8,128]{3,1,2,0:T(1,128)S(1)}, f32[1,1,8,128]{3,1,2,0:T(1,128)S(1)}, u32[]{:S(2)}, u32[]{:S(2)}) %collective-permute-start.9) | collective-permute-done | bytes 4128 | tf_op jit(solution)/shard_map/ppermute | solution.py:36
  38.6 0.5 collective-permute-start.11
  39.2 0.7 collective-permute-done.10
  39.9 1.8 %collective-permute-done.11 = f32[1,8,1,128]{3,1,2,0:T(8,128)S(1)} collective-permute-done((f32[1,8,1,128]{3,1,2,0:T(8,128)S(1)}, f32[1,8,1,128]{3,1,2,0:T(8,128)S(1)}, u32[]{:S(2)}, u32[]{:S(2)}) %collective-permute-start.11) | collective-permute-done | bytes 4128 | tf_op jit(solution)/shard_map/ppermute | solution.py:36
  42.1 0.5 copy-done.8
  43.0 0.6 copy-done.11
  44.0 2.0 %collective-permute-start.13 = (f32[2,1,8,128]{3,1,2,0:T(1,128)S(1)}, f32[2,1,8,128]{3,1,2,0:T(1,128)S(1)}, u32[]{:S(2)}, u32[]{:S(2)}) collective-permute-start(f32[2,1,8,128]{3,1,2,0:T(1,128)S(1)} %get-tuple-element.30), channel_id=1, source_target_pairs={{0,4},{4,8},{8,12},{12,16},{16,20},{20,24},{24,28},{28,0},{1,5},{5... | collective-permute-start | bytes 24584 | tf_op jit(solution)/shard_map/ppermute | solution.py:36
  46.0 1.6 collective-permute-done.12
  47.6 2.8 %collective-permute-done.13 = f32[2,1,8,128]{3,1,2,0:T(1,128)S(1)} collective-permute-done((f32[2,1,8,128]{3,1,2,0:T(1,128)S(1)}, f32[2,1,8,128]{3,1,2,0:T(1,128)S(1)}, u32[]{:S(2)}, u32[]{:S(2)}) %collective-permute-start.13) | collective-permute-done | bytes 8224 | tf_op jit(solution)/shard_map/ppermute | solution.py:36
  50.5 0.5 collective-permute-start.15
  51.0 0.9 collective-permute-done.14
  51.9 1.8 %collective-permute-done.15 = f32[2,8,1,128]{3,1,2,0:T(8,128)S(1)} collective-permute-done((f32[2,8,1,128]{3,1,2,0:T(8,128)S(1)}, f32[2,8,1,128]{3,1,2,0:T(8,128)S(1)}, u32[]{:S(2)}, u32[]{:S(2)}) %collective-permute-start.15) | collective-permute-done | bytes 8224 | tf_op jit(solution)/shard_map/ppermute | solution.py:36
  54.8 0.6 copy-done.4
  55.8 0.7 copy-done.3
  56.8 2.0 %collective-permute-start.17 = (f32[1,1,8,128]{3,1,2,0:T(1,128)S(1)}, f32[1,1,8,128]{3,1,2,0:T(1,128)S(1)}, u32[]{:S(2)}, u32[]{:S(2)}) collective-permute-start(f32[1,1,8,128]{3,1,2,0:T(1,128)S(1)} %get-tuple-element.46), channel_id=1, source_target_pairs={{0,4},{4,8},{8,12},{12,16},{16,20},{20,24},{24,28},{28,0},{1,5},{5... | collective-permute-start | bytes 12296 | tf_op jit(solution)/shard_map/ppermute | solution.py:36
  58.8 1.6 collective-permute-done.16
  60.4 2.8 %collective-permute-done.17 = f32[1,1,8,128]{3,1,2,0:T(1,128)S(1)} collective-permute-done((f32[1,1,8,128]{3,1,2,0:T(1,128)S(1)}, f32[1,1,8,128]{3,1,2,0:T(1,128)S(1)}, u32[]{:S(2)}, u32[]{:S(2)}) %collective-permute-start.17) | collective-permute-done | bytes 4128 | tf_op jit(solution)/shard_map/ppermute | solution.py:36
  63.8 0.8 collective-permute-done.18
  64.6 1.8 %collective-permute-done.19 = f32[1,8,1,128]{3,1,2,0:T(8,128)S(1)} collective-permute-done((f32[1,8,1,128]{3,1,2,0:T(8,128)S(1)}, f32[1,8,1,128]{3,1,2,0:T(8,128)S(1)}, u32[]{:S(2)}, u32[]{:S(2)}) %collective-permute-start.19) | collective-permute-done | bytes 4128 | tf_op jit(solution)/shard_map/ppermute | solution.py:36
  66.6 0.7 fusion.105
  67.3 37.1 %all-reduce.1 = (f32[]{:T(128)}, f32[]{:T(128)}) all-reduce(f32[]{:T(128)} %get-tuple-element.9, f32[]{:T(128)} %get-tuple-element.8), channel_id=1, replica_groups=mesh['dom'=8,'sub'=4] {'dom','sub'}, use_global_device_ids=true, to_apply=%region_1.2 | all-reduce | flops 2 | bytes 16 | tf_op jit(solution)/shard_map/psum | solution.py:138
  107.1 4.0 %collective-permute-start.20 = (f32[1,1,8,128]{3,1,2,0:T(1,128)S(1)}, f32[1,1,8,128]{3,1,2,0:T(1,128)S(1)}, u32[]{:S(2)}, u32[]{:S(2)}) collective-permute-start(f32[1,1,8,128]{3,1,2,0:T(1,128)S(1)} %get-tuple-element.37), channel_id=1, source_target_pairs={{4,0},{8,4},{12,8},{16,12},{20,16},{24,20},{28,24},{0,28},{5,1},{9... | collective-permute-start | bytes 12296 | tf_op jit(solution)/shard_map/ppermute | solution.py:37
  111.1 1.3 collective-permute-done.20
  112.4 5.0 %collective-permute-done.21 = f32[1,1,8,128]{3,1,2,0:T(1,128)S(1)} collective-permute-done((f32[1,1,8,128]{3,1,2,0:T(1,128)S(1)}, f32[1,1,8,128]{3,1,2,0:T(1,128)S(1)}, u32[]{:S(2)}, u32[]{:S(2)}) %collective-permute-start.21) | collective-permute-done | bytes 4128 | tf_op jit(solution)/shard_map/ppermute | solution.py:36
  118.1 0.6 copy.103
  118.9 1.8 %collective-permute-done.23 = f32[1,8,1,128]{3,1,2,0:T(8,128)S(1)} collective-permute-done((f32[1,8,1,128]{3,1,2,0:T(8,128)S(1)}, f32[1,8,1,128]{3,1,2,0:T(8,128)S(1)}, u32[]{:S(2)}, u32[]{:S(2)}) %collective-permute-start.23) | collective-permute-done | bytes 4128 | tf_op jit(solution)/shard_map/ppermute | solution.py:36
  120.9 0.8 fusion.107
  121.7 37.4 %all-reduce = (f32[]{:T(128)}, f32[]{:T(128)}) all-reduce(f32[]{:T(128)} %get-tuple-element.7, f32[]{:T(128)} %get-tuple-element.6), channel_id=1, replica_groups=mesh['dom'=8,'sub'=4] {'dom','sub'}, use_global_device_ids=true, to_apply=%region_5.6 | all-reduce | flops 2 | bytes 16 | tf_op jit(solution)/shard_map/psum | solution.py:138
  163.6 0.6 copy.105
  164.2 0.6 copy.104
  (120 shorter events, 10.8 us)
Async XLA Ops:
  0.6 0.8 copy-start.1
  0.6 0.8 copy-start.2
  1.6 0.8 copy-start
  2.7 7.4 %collective-permute-start = (f32[1,1,8,128]{3,1,2,0:T(1,128)S(1)}, f32[1,1,8,128]{3,1,2,0:T(1,128)S(1)}, u32[]{:S(2)}, u32[]{:S(2)}) collective-permute-start(f32[1,1,8,128]{3,1,2,0:T(1,128)S(1)} %get-tuple-element.73), channel_id=1, source_target_pairs={{4,0},{8,4},{12,8},{16,12},{20,16},{24,20},{28,24},{0,28},{5,1},{9... | collective-permute-start | bytes 12296 | tf_op jit(solution)/shard_map/ppermute | solution.py:37
  8.8 6.3 %collective-permute-start.1 = (f32[1,1,8,128]{3,1,2,0:T(1,128)S(1)}, f32[1,1,8,128]{3,1,2,0:T(1,128)S(1)}, u32[]{:S(2)}, u32[]{:S(2)}) collective-permute-start(f32[1,1,8,128]{3,1,2,0:T(1,128)S(1)} %get-tuple-element.74), channel_id=1, source_target_pairs={{0,4},{4,8},{8,12},{12,16},{16,20},{20,24},{24,28},{28,0},{1,5},{5... | collective-permute-start | bytes 12296 | tf_op jit(solution)/shard_map/ppermute | solution.py:36
  8.8 0.7 copy-start.10
  15.2 1.4 collective-permute-start.2
  15.3 3.1 %collective-permute-start.3 = (f32[1,8,1,128]{3,1,2,0:T(8,128)S(1)}, f32[1,8,1,128]{3,1,2,0:T(8,128)S(1)}, u32[]{:S(2)}, u32[]{:S(2)}) collective-permute-start(f32[1,8,1,128]{3,1,2,0:T(8,128)S(1)} %get-tuple-element.72), channel_id=1, source_target_pairs={{0,1},{1,2},{2,3},{3,0},{4,5},{5,6},{6,7},{7,4},{8,9},{9,10},{10,1... | collective-permute-start | bytes 12296 | tf_op jit(solution)/shard_map/ppermute | solution.py:36
  18.6 0.7 copy-start.6
  20.7 3.7 %collective-permute-start.4 = (f32[1,1,8,128]{3,1,2,0:T(1,128)S(1)}, f32[1,1,8,128]{3,1,2,0:T(1,128)S(1)}, u32[]{:S(2)}, u32[]{:S(2)}) collective-permute-start(f32[1,1,8,128]{3,1,2,0:T(1,128)S(1)} %get-tuple-element.61), channel_id=1, source_target_pairs={{4,0},{8,4},{12,8},{16,12},{20,16},{24,20},{28,24},{0,28},{5,1},{9... | collective-permute-start | bytes 12296 | tf_op jit(solution)/shard_map/ppermute | solution.py:37
  20.7 6.4 %collective-permute-start.5 = (f32[1,1,8,128]{3,1,2,0:T(1,128)S(1)}, f32[1,1,8,128]{3,1,2,0:T(1,128)S(1)}, u32[]{:S(2)}, u32[]{:S(2)}) collective-permute-start(f32[1,1,8,128]{3,1,2,0:T(1,128)S(1)} %get-tuple-element.62), channel_id=1, source_target_pairs={{0,4},{4,8},{8,12},{12,16},{16,20},{20,24},{24,28},{28,0},{1,5},{5... | collective-permute-start | bytes 12296 | tf_op jit(solution)/shard_map/ppermute | solution.py:36
  27.2 1.4 collective-permute-start.6
  27.3 3.1 %collective-permute-start.7 = (f32[1,8,1,128]{3,1,2,0:T(8,128)S(1)}, f32[1,8,1,128]{3,1,2,0:T(8,128)S(1)}, u32[]{:S(2)}, u32[]{:S(2)}) collective-permute-start(f32[1,8,1,128]{3,1,2,0:T(8,128)S(1)} %get-tuple-element.60), channel_id=1, source_target_pairs={{0,1},{1,2},{2,3},{3,0},{4,5},{5,6},{6,7},{7,4},{8,9},{9,10},{10,1... | collective-permute-start | bytes 12296 | tf_op jit(solution)/shard_map/ppermute | solution.py:36
  32.0 2.1 %copy-start.9 = (f32[8]{0:T(128)S(1)}, f32[8]{0:T(128)}, u32[]{:S(2)}) copy-start(f32[8]{0:T(128)} %constant.109.clone) | copy-start | bytes 100
  32.0 3.7 %collective-permute-start.8 = (f32[1,1,8,128]{3,1,2,0:T(1,128)S(1)}, f32[1,1,8,128]{3,1,2,0:T(1,128)S(1)}, u32[]{:S(2)}, u32[]{:S(2)}) collective-permute-start(f32[1,1,8,128]{3,1,2,0:T(1,128)S(1)} %get-tuple-element.53), channel_id=1, source_target_pairs={{4,0},{8,4},{12,8},{16,12},{20,16},{24,20},{28,24},{0,28},{5,1},{9... | collective-permute-start | bytes 12296 | tf_op jit(solution)/shard_map/ppermute | solution.py:37
  32.1 6.4 %collective-permute-start.9 = (f32[1,1,8,128]{3,1,2,0:T(1,128)S(1)}, f32[1,1,8,128]{3,1,2,0:T(1,128)S(1)}, u32[]{:S(2)}, u32[]{:S(2)}) collective-permute-start(f32[1,1,8,128]{3,1,2,0:T(1,128)S(1)} %get-tuple-element.54), channel_id=1, source_target_pairs={{0,4},{4,8},{8,12},{12,16},{16,20},{20,24},{24,28},{28,0},{1,5},{5... | collective-permute-start | bytes 12296 | tf_op jit(solution)/shard_map/ppermute | solution.py:36
  34.1 4.9 %copy-start.5 = (f32[8,8,128]{2,1,0:T(8,128)S(1)}, f32[8,8,128]{2,1,0:T(8,128)}, u32[]{:S(2)}) copy-start(f32[8,8,128]{2,1,0:T(8,128)} %param.41) | copy-start | bytes 98308
  38.5 0.7 copy-start.7
  38.5 1.4 collective-permute-start.10
  38.6 3.1 %collective-permute-start.11 = (f32[1,8,1,128]{3,1,2,0:T(8,128)S(1)}, f32[1,8,1,128]{3,1,2,0:T(8,128)S(1)}, u32[]{:S(2)}, u32[]{:S(2)}) collective-permute-start(f32[1,8,1,128]{3,1,2,0:T(8,128)S(1)} %get-tuple-element.52), channel_id=1, source_target_pairs={{0,1},{1,2},{2,3},{3,0},{4,5},{5,6},{6,7},{7,4},{8,9},{9,10},{10,1... | collective-permute-start | bytes 12296 | tf_op jit(solution)/shard_map/ppermute | solution.py:36
  41.9 0.7 copy-start.8
  42.8 0.8 copy-start.11
  43.9 3.7 %collective-permute-start.12 = (f32[2,1,8,128]{3,1,2,0:T(1,128)S(1)}, f32[2,1,8,128]{3,1,2,0:T(1,128)S(1)}, u32[]{:S(2)}, u32[]{:S(2)}) collective-permute-start(f32[2,1,8,128]{3,1,2,0:T(1,128)S(1)} %get-tuple-element.29), channel_id=1, source_target_pairs={{4,0},{8,4},{12,8},{16,12},{20,16},{24,20},{28,24},{0,28},{5,1},{9... | collective-permute-start | bytes 24584 | tf_op jit(solution)/shard_map/ppermute | solution.py:37
  44.0 6.4 %collective-permute-start.13 = (f32[2,1,8,128]{3,1,2,0:T(1,128)S(1)}, f32[2,1,8,128]{3,1,2,0:T(1,128)S(1)}, u32[]{:S(2)}, u32[]{:S(2)}) collective-permute-start(f32[2,1,8,128]{3,1,2,0:T(1,128)S(1)} %get-tuple-element.30), channel_id=1, source_target_pairs={{0,4},{4,8},{8,12},{12,16},{16,20},{20,24},{24,28},{28,0},{1,5},{5... | collective-permute-start | bytes 24584 | tf_op jit(solution)/shard_map/ppermute | solution.py:36
  50.5 1.4 collective-permute-start.14
  50.5 3.2 %collective-permute-start.15 = (f32[2,8,1,128]{3,1,2,0:T(8,128)S(1)}, f32[2,8,1,128]{3,1,2,0:T(8,128)S(1)}, u32[]{:S(2)}, u32[]{:S(2)}) collective-permute-start(f32[2,8,1,128]{3,1,2,0:T(8,128)S(1)} %get-tuple-element.28), channel_id=1, source_target_pairs={{0,1},{1,2},{2,3},{3,0},{4,5},{5,6},{6,7},{7,4},{8,9},{9,10},{10,1... | collective-permute-start | bytes 24584 | tf_op jit(solution)/shard_map/ppermute | solution.py:36
  54.7 0.7 copy-start.4
  55.6 0.9 copy-start.3
  56.7 3.7 %collective-permute-start.16 = (f32[1,1,8,128]{3,1,2,0:T(1,128)S(1)}, f32[1,1,8,128]{3,1,2,0:T(1,128)S(1)}, u32[]{:S(2)}, u32[]{:S(2)}) collective-permute-start(f32[1,1,8,128]{3,1,2,0:T(1,128)S(1)} %get-tuple-element.45), channel_id=1, source_target_pairs={{4,0},{8,4},{12,8},{16,12},{20,16},{24,20},{28,24},{0,28},{5,1},{9... | collective-permute-start | bytes 12296 | tf_op jit(solution)/shard_map/ppermute | solution.py:37
  56.8 6.4 %collective-permute-start.17 = (f32[1,1,8,128]{3,1,2,0:T(1,128)S(1)}, f32[1,1,8,128]{3,1,2,0:T(1,128)S(1)}, u32[]{:S(2)}, u32[]{:S(2)}) collective-permute-start(f32[1,1,8,128]{3,1,2,0:T(1,128)S(1)} %get-tuple-element.46), channel_id=1, source_target_pairs={{0,4},{4,8},{8,12},{12,16},{16,20},{20,24},{24,28},{28,0},{1,5},{5... | collective-permute-start | bytes 12296 | tf_op jit(solution)/shard_map/ppermute | solution.py:36
  63.2 1.4 collective-permute-start.18
  63.3 3.1 %collective-permute-start.19 = (f32[1,8,1,128]{3,1,2,0:T(8,128)S(1)}, f32[1,8,1,128]{3,1,2,0:T(8,128)S(1)}, u32[]{:S(2)}, u32[]{:S(2)}) collective-permute-start(f32[1,8,1,128]{3,1,2,0:T(8,128)S(1)} %get-tuple-element.44), channel_id=1, source_target_pairs={{0,1},{1,2},{2,3},{3,0},{4,5},{5,6},{6,7},{7,4},{8,9},{9,10},{10,1... | collective-permute-start | bytes 12296 | tf_op jit(solution)/shard_map/ppermute | solution.py:36
  107.1 5.4 %collective-permute-start.20 = (f32[1,1,8,128]{3,1,2,0:T(1,128)S(1)}, f32[1,1,8,128]{3,1,2,0:T(1,128)S(1)}, u32[]{:S(2)}, u32[]{:S(2)}) collective-permute-start(f32[1,1,8,128]{3,1,2,0:T(1,128)S(1)} %get-tuple-element.37), channel_id=1, source_target_pairs={{4,0},{8,4},{12,8},{16,12},{20,16},{24,20},{28,24},{0,28},{5,1},{9... | collective-permute-start | bytes 12296 | tf_op jit(solution)/shard_map/ppermute | solution.py:37
  111.1 6.3 %collective-permute-start.21 = (f32[1,1,8,128]{3,1,2,0:T(1,128)S(1)}, f32[1,1,8,128]{3,1,2,0:T(1,128)S(1)}, u32[]{:S(2)}, u32[]{:S(2)}) collective-permute-start(f32[1,1,8,128]{3,1,2,0:T(1,128)S(1)} %get-tuple-element.38), channel_id=1, source_target_pairs={{0,4},{4,8},{8,12},{12,16},{16,20},{20,24},{24,28},{28,0},{1,5},{5... | collective-permute-start | bytes 12296 | tf_op jit(solution)/shard_map/ppermute | solution.py:36
  117.5 1.4 collective-permute-start.22
  117.6 3.1 %collective-permute-start.23 = (f32[1,8,1,128]{3,1,2,0:T(8,128)S(1)}, f32[1,8,1,128]{3,1,2,0:T(8,128)S(1)}, u32[]{:S(2)}, u32[]{:S(2)}) collective-permute-start(f32[1,8,1,128]{3,1,2,0:T(8,128)S(1)} %get-tuple-element.36), channel_id=1, source_target_pairs={{0,1},{1,2},{2,3},{3,0},{4,5},{5,6},{6,7},{7,4},{8,9},{9,10},{10,1... | collective-permute-start | bytes 12296 | tf_op jit(solution)/shard_map/ppermute | solution.py:36
where the time goes:
time: 166 us; the launch traced here: 165 us
  blocking collectives  74.4 us (45%)
  waiting for transfers between devices  44.1 us (27%)
  starting transfers between devices  21.7 us (13%)
  local copies, waits for them, and re-layouts  8.15 us (5%)
  between operations  7.07 us (4%)
  matrix products  5.75 us (3%)
  other arithmetic  3.65 us (2%)
    psum x2, blocking collectives, both_sums(): lax.psum((jnp.sum(residual * precond * inv_mult), jnp.sum(precond * appli...  74.4 us
    ppermute x12, waiting for transfers between devices, padded(): before = lax.ppermute(last, axis, up)  31.7 us
    ppermute x12, waiting for transfers between devices, padded(): after = lax.ppermute(leading, axis, down)  12.4 us
    ppermute x12, starting transfers between devices, padded(): before = lax.ppermute(last, axis, up)  11 us
    ppermute x12, starting transfers between devices, padded(): after = lax.ppermute(leading, axis, down)  10.7 us
    unnamed x27, local copies, waits for them, and re-layouts  6.38 us
  transfers between devices with their start and end apart: 24, of which 24 were waited for; matrix products, arithmetic and copies ran while one was open for 1% of the time, Pallas kernels for 0%

commit v1 on v0

v1 whole, which is shorter than its diff:
```python
import functools

import jax
import jax.numpy as jnp
import numpy as np
from jax import lax
from jax.experimental import pallas as pl
from jax.experimental.pallas import tpu as pltpu
from jax.sharding import PartitionSpec as P

SWEEPS = 2
PITERS = 2
MESH = pl.DeviceIdType.MESH


gll_nodes = [
    -1.0,
    -0.8717401485096066,
    -0.5917001814331423,
    -0.2092992179024789,
    0.2092992179024789,
    0.5917001814331423,
    0.8717401485096066,
    1.0,
]
advect_step = 0.05
reinit_step = 0.02
interface_width = 0.1
density_ratio = 9.0
ORDER = 8
GRAD, TRANS, SQUARE = 0, 1, 2


def tables():
    node_points = np.array(gll_nodes)
    poly_order = 7
    values_prev = np.ones(8)
    values_now = node_points.copy()
    for degree in range(1, poly_order):
        values_next = ((2 * degree + 1) * node_points * values_now - degree * values_prev) / (
            degree + 1
        )
        values_prev, values_now = (values_now, values_next)
    matrix = np.zeros((8, 8))
    for line in range(8):
        for column in range(8):
            if line != column:
                matrix[line, column] = values_now[line] / (
                    values_now[column] * (node_points[line] - node_points[column])
                )
    matrix[0, 0] = -poly_order * (poly_order + 1) / 4.0
    matrix[7, 7] = poly_order * (poly_order + 1) / 4.0
    weights = 2.0 / (poly_order * (poly_order + 1) * values_now**2)
    return (matrix, weights)


MATRIX, WEIGHTS = tables()
KINDS = (MATRIX, MATRIX.T, (MATRIX * MATRIX).T)
COUNT = np.array([0.5, 1.0, 1.0, 1.0, 1.0, 1.0, 1.0, 0.5])


def constants(lanes):
    rows = np.arange(ORDER)
    planes = []
    for matrix in KINDS:
        for shift in range(ORDER):
            column = matrix[rows, (rows - shift) % ORDER]
            planes.append(np.broadcast_to(column[:, None], (ORDER, lanes)))
    repeats = lanes // ORDER
    planes.append(WEIGHTS[:, None] * np.tile(WEIGHTS, repeats)[None, :])
    planes.append(COUNT[:, None] * np.tile(COUNT, repeats)[None, :])
    planes = np.stack(planes).astype(np.float32)
    wide = []
    for matrix in KINDS:
        full = np.kron(np.eye(repeats), matrix.T).astype(np.float32)
        high = full.astype(jnp.bfloat16)
        low = (full - high.astype(np.float32)).astype(jnp.bfloat16)
        wide.append(np.concatenate([high, low], axis=1))
    return planes, np.stack(wide)


def along_first(values, kind):
    matrix = KINDS[kind]
    half = ORDER // 2
    flip = -1.0 if kind != SQUARE else 1.0
    even = [values[i] + values[ORDER - 1 - i] for i in range(half)]
    odd = [values[i] - values[ORDER - 1 - i] for i in range(half)]
    front, back = [], []
    for j in range(half):
        even_sum = odd_sum = None
        for i in range(half):
            ce = float(0.5 * (matrix[j, i] + matrix[j, ORDER - 1 - i]))
            co = float(0.5 * (matrix[j, i] - matrix[j, ORDER - 1 - i]))
            even_sum = even[i] * ce if even_sum is None else even_sum + even[i] * ce
            odd_sum = odd[i] * co if odd_sum is None else odd_sum + odd[i] * co
        front.append(even_sum + odd_sum)
        back.append(flip * (even_sum - odd_sum))
    return front + back[::-1]


def kernel(ndom, nsub, local_barrier, level_ref, velocity_ref, source_ref, planes_ref, wide_ref,
           new_ref, pressure_ref, correction_ref, *scratch):
    (level_v, velocity_v, source_v, planes_v, wide_v, out_v, in_sem, out_sem,
     face_send, face_recv, edge_send, edge_recv, sum_send, sum_recv,
     first_faces, first_edges, first_faces_in, first_edges_in,
     faces, edges, faces_in, edges_in, sums, sums_in) = scratch
    dom, sub = lax.axis_index("dom"), lax.axis_index("sub")

    def peer(a, b):
        return (lax.rem(dom + a % ndom, ndom), lax.rem(sub + b % nsub, nsub))

    loads = [
        pltpu.make_async_copy(src, dst, in_sem.at[i])
        for i, (src, dst) in enumerate((
            (level_ref, level_v), (planes_ref, planes_v), (wide_ref, wide_v),
            (velocity_ref, velocity_v), (source_ref, source_v)))
    ]
    barrier = pltpu.get_barrier_semaphore()
    near = [(a, b) for a in (-1, 1, 0) for b in (-1, 1, 0) if a or b]
    if local_barrier:
        for a, b in near:
            pl.semaphore_signal(barrier, inc=1, device_id=peer(a, b), device_id_type=MESH)
    else:
        @pl.loop(1, ndom * nsub)
        def _(k):
            target = (lax.rem(dom + k // nsub, ndom), lax.rem(sub + k % nsub, nsub))
            pl.semaphore_signal(barrier, inc=1, device_id=target, device_id_type=MESH)
    for load in loads:
        load.start()

    shape = level_v.shape[1:]
    lane = lax.broadcasted_iota(jnp.int32, shape, 1) % ORDER
    row = lax.broadcasted_iota(jnp.int32, shape, 0)
    lane_first, lane_last = lane == 0, lane == ORDER - 1
    row_first, row_last = row == 0, row == ORDER - 1
    lanes = shape[1]
    span = range(ORDER)

    def fold_lanes(v):
        lower = pltpu.roll(v, 1, 1)
        upper = pltpu.roll(v, lanes - 1, 1)
        return v + jnp.where(lane_last, upper, jnp.where(lane_first, lower, 0.0))

    def along_second(values, kind):
        result = []
        for v in values:
            total = v * planes_v[kind * ORDER]
            for shift in range(1, ORDER):
                total = total + pltpu.roll(v, shift, 0) * planes_v[kind * ORDER + shift]
            result.append(total)
        return result

    def along_third(values, kind):
        stacked = jnp.concatenate(values, axis=0)
        high = stacked.astype(jnp.bfloat16)
        low = (stacked - high.astype(jnp.float32)).astype(jnp.bfloat16)
        out = jnp.dot(jnp.concatenate([high, low], axis=0), wide_v[kind],
                      preferred_element_type=jnp.float32)
        n = ORDER * ORDER
        total = out[:n, :lanes] + (out[:n, lanes:] + out[n:, :lanes])
        return [total[i * ORDER:(i + 1) * ORDER] for i in span]

    def gradient(values):
        third = along_third(values, GRAD)
        return along_first(values, GRAD), along_second(values, GRAD), third

    def divergence(parts, kind):
        third = along_third(parts[2], kind)
        first, second = along_first(parts[0], kind), along_second(parts[1], kind)
        return [(first[i] + second[i]) + third[i] for i in span]

    def send(slot, fields, face_out, edge_out, face_in, edge_in):
        fields = [[fold_lanes(v) for v in field] for field in fields]
        for n, field in enumerate(fields):
            face_out[0, n] = field[ORDER - 1]
            face_out[1, n] = field[0]
            right = jnp.concatenate([v[ORDER - 1:] for v in field], axis=0)
            left = jnp.concatenate([v[:1] for v in field], axis=0)
            face_out[2, n] = right
            face_out[3, n] = left
            edge_out[0, n] = field[ORDER - 1][ORDER - 1:]
            edge_out[1, n] = field[ORDER - 1][:1]
            edge_out[2, n] = field[0][ORDER - 1:]
            edge_out[3, n] = field[0][:1]
        for i, (a, b) in enumerate(((1, 1), (1, -1), (-1, 1), (-1, -1))):
            pltpu.make_async_remote_copy(
                edge_out.at[i], edge_in.at[i], edge_send.at[slot], edge_recv.at[slot],
                device_id=peer(a, b), device_id_type=MESH).start()
        for i, (a, b) in enumerate(((1, 0), (-1, 0), (0, 1), (0, -1))):
            pltpu.make_async_remote_copy(
                face_out.at[i], face_in.at[i], face_send.at[slot], face_recv.at[slot],
                device_id=peer(a, b), device_id_type=MESH).start()
        return fields

    def receive(slot, fields, face_in, edge_in):
        pltpu.make_async_copy(face_in, face_in, face_recv.at[slot]).wait()
        pltpu.make_async_copy(edge_in, edge_in, edge_recv.at[slot]).wait()
        results = []
        for n, field in enumerate(fields):
            result = list(field)
            result[0] = result[0] + face_in[0, n]
            result[ORDER - 1] = result[ORDER - 1] + face_in[1, n]
            for i, (at, mask_a, mask_b) in enumerate((
                    (0, row_first, row_last), (ORDER - 1, row_first, row_last))):
                result[at] = result[at] + jnp.where(
                    mask_a, edge_in[2 * i, n],
                    jnp.where(mask_b, edge_in[2 * i + 1, n], 0.0))
            for i in span:
                result[i] = result[i] + jnp.where(
                    row_first, face_in[2, n, i:i + 1],
                    jnp.where(row_last, face_in[3, n, i:i + 1], 0.0))
            results.append(result)
        return results

    def begin(step, field):
        buffers = (faces.at[step], edges.at[step], faces_in.at[step], edges_in.at[step])
        return send(step + 1, [field], *buffers)

    def finish(step, field):
        return receive(step + 1, field, faces_in.at[step], edges_in.at[step])[0]

    def assemble(step, field):
        return finish(step, begin(step, field))

    hops = sorted(range(ndom), key=lambda a: -min(a, ndom - a))
    others = [(a, b) for a in hops for b in (2, 1, 3, 0) if a or b] if nsub == 4 else [
        (a, b) for a in hops for b in range(nsub) if a or b]

    def begin_sums(step, first, second):
        sums[step, 0:1] = jnp.sum(first, axis=0, keepdims=True)
        sums[step, 1:2] = jnp.sum(second, axis=0, keepdims=True)

        def post(target, k):
            pltpu.make_async_remote_copy(
                sums.at[step], sums_in.at[step, k], sum_send.at[step], sum_recv.at[step],
                device_id=target, device_id_type=MESH).start()
        if ndom * nsub <= 64:
            for k, (a, b) in enumerate(others):
                post(peer(a, b), k)
        else:
            @pl.loop(1, ndom * nsub)
            def _(k):
                post((lax.rem(dom + k // nsub, ndom), lax.rem(sub + k % nsub, nsub)), k - 1)

    def finish_sums(step):
        pltpu.make_async_copy(sums_in.at[step], sums_in.at[step], sum_recv.at[step]).wait()
        total = sums[step] + jnp.sum(sums_in[step], axis=0)
        total = jnp.sum(total, axis=1, keepdims=True)
        return total[0:1], total[1:2]

    def dot(a, b, scale=None):
        total = None
        for i in span:
            term = a[i] * b[i]
            if scale is not None:
                term = term * scale[i]
            total = term if total is None else total + term
        return total

    for load in loads[:3]:
        load.wait()
    weight_plane = planes_v[3 * ORDER]
    count_plane = planes_v[3 * ORDER + 1]
    weight = [weight_plane * float(WEIGHTS[i]) for i in span]
    inv_mult = [count_plane * float(COUNT[i]) for i in span]

    phi = [level_v[i] for i in span]
    g0, g1, g2 = gradient(phi)
    loads[3].wait()
    advected = [
        phi[i] - advect_step * (velocity_v[0, i] * g0[i] + velocity_v[1, i] * g1[i]
                                + velocity_v[2, i] * g2[i]) for i in span]
    loads[4].wait()
    right = [weight[i] * source_v[i] for i in span]
    pl.semaphore_wait(barrier, len(near) if local_barrier else ndom * nsub - 1)
    fields = send(0, [advected, right], first_faces, first_edges, first_faces_in, first_edges_in)
    phi, right = receive(0, fields, first_faces_in, first_edges_in)
    phi = [phi[i] * inv_mult[i] for i in span]

    step = 0
    for sweep in range(SWEEPS):
        g0, g1, g2 = gradient(phi)
        if sweep == 0:
            scaled = [lax.rsqrt(jnp.maximum(
                g0[i] * g0[i] + g1[i] * g1[i] + g2[i] * g2[i], 1.0)) for i in span]
            normals = [[g[i] * scaled[i] for i in span] for g in (g0, g1, g2)]
        compress = [p * (1.0 - p) for p in phi]
        flux = [[interface_width * g[i] - compress[i] * normal[i] for i in span]
                for g, normal in zip((g0, g1, g2), normals)]
        change = assemble(step, divergence(flux, GRAD))
        step += 1
        phi = [phi[i] + reinit_step * change[i] * inv_mult[i] for i in span]

    for i in span:
        out_v[0, i] = phi[i]
    stores = [pltpu.make_async_copy(out_v.at[n], ref, out_sem.at[n])
              for n, ref in enumerate((new_ref, pressure_ref, correction_ref))]
    stores[0].start()
    weighted = [weight[i] * (1.0 / (1.0 + density_ratio * phi[i] * phi[i])) for i in span]
    squares = divergence([weighted] * 3, SQUARE)
    diagonal = assemble(step, [weight[i] + squares[i] for i in span])
    step += 1
    inverse = [1.0 / v for v in diagonal]

    def operate(values):
        parts = [[weighted[i] * g[i] for i in span] for g in gradient(values)]
        total = divergence(parts, TRANS)
        return [weight[i] * values[i] + total[i] for i in span]

    def apply(step, sum_step, residual, precond):
        partial = operate(precond)
        sent = begin(step, partial)
        begin_sums(sum_step, dot(residual, precond, inv_mult), dot(precond, partial))
        applied = finish(step, sent)
        return (applied,) + finish_sums(sum_step)

    residual = right
    precond = [residual[i] * inverse[i] for i in span]
    applied, norm_now, product = apply(step, 0, residual, precond)
    step += 1
    step_size = norm_now / product
    direction, image = precond, applied
    result = None
    for it in range(PITERS):
        moved = [step_size * d for d in direction]
        result = moved if result is None else [result[i] + moved[i] for i in span]
        residual = [residual[i] - step_size * image[i] for i in span]
        if it + 1 < PITERS:
            precond = [residual[i] * inverse[i] for i in span]
            applied, norm_next, product = apply(step, it + 1, residual, precond)
            step += 1
            ratio = norm_next / norm_now
            step_size = norm_next / (product - ratio * norm_next / step_size)
            direction = [precond[i] + ratio * direction[i] for i in span]
            image = [applied[i] + ratio * image[i] for i in span]
            norm_now = norm_next
    for i in span:
        out_v[1, i] = result[i]
        out_v[2, i] = residual[i] * inverse[i]
    stores[1].start()
    stores[2].start()
    pltpu.make_async_copy(first_faces, first_faces, face_send.at[0]).wait()
    pltpu.make_async_copy(first_edges, first_edges, edge_send.at[0]).wait()
    for s in range(step):
        pltpu.make_async_copy(faces.at[s], faces.at[s], face_send.at[s + 1]).wait()
        pltpu.make_async_copy(edges.at[s], edges.at[s], edge_send.at[s + 1]).wait()
    for s in range(PITERS):
        pltpu.make_async_copy(sums_in.at[s], sums_in.at[s], sum_send.at[s]).wait()
    for store in stores:
        store.wait()


def solution(mesh):
    ndom, nsub = mesh.shape["dom"], mesh.shape["sub"]
    rounds = SWEEPS + 1 + PITERS
    local_barrier = max(ndom, nsub) // 2 <= SWEEPS + 3

    def local(level_set, velocity, source):
        assert level_set.shape[:2] == (ORDER, ORDER)
        lanes = level_set.shape[2]
        planes, wide = constants(lanes)
        tile = (ORDER, lanes)
        vmem = functools.partial(pltpu.VMEM, dtype=jnp.float32)
        others = ndom * nsub - 1
        dma = pltpu.SemaphoreType.DMA
        scratch = [
            vmem(level_set.shape), vmem(velocity.shape), vmem(source.shape),
            vmem(planes.shape), pltpu.VMEM(wide.shape, jnp.bfloat16),
            vmem((3,) + level_set.shape), dma((5,)), dma((3,)),
            dma((rounds + 1,)), dma((rounds + 1,)), dma((rounds + 1,)), dma((rounds + 1,)),
            dma((PITERS,)), dma((PITERS,)),
            vmem((4, 2) + tile), vmem((4, 2, 1, lanes)),
            vmem((4, 2) + tile), vmem((4, 2, 1, lanes)),
            vmem((rounds, 4, 1) + tile), vmem((rounds, 4, 1, 1, lanes)),
            vmem((rounds, 4, 1) + tile), vmem((rounds, 4, 1, 1, lanes)),
            vmem((PITERS, 2, lanes)), vmem((PITERS, others, 2, lanes)),
        ]
        any_space = pl.BlockSpec(memory_space=pl.ANY)
        out = jax.ShapeDtypeStruct(level_set.shape, jnp.float32)
        return pl.pallas_call(
            functools.partial(kernel, ndom, nsub, local_barrier),
            out_shape=(out, out, out),
            in_specs=[any_space] * 5,
            out_specs=(any_space,) * 3,
            scratch_shapes=scratch,
            compiler_params=pltpu.CompilerParams(collective_id=0, has_side_effects=True),
        )(level_set, velocity, source, jnp.asarray(planes), jnp.asarray(wide))

    return jax.shard_map(
        local,
        mesh=mesh,
        in_specs=(P("dom", "sub", None), P(None, "dom", "sub", None), P("dom", "sub", None)),
        out_specs=(P("dom", "sub", None), P("dom", "sub", None), P("dom", "sub", None)),
        check_vma=False,
    )
```

time: 166 us -> 38.7 us (0.23)
  blocking collectives: 74.4 us -> 0 us
  waiting for transfers between devices: 44.1 us -> 0 us
  Pallas kernels: 0 us -> 35 us
  starting transfers between devices: 21.7 us -> 0 us
  between operations: 7.07 us -> 0.65 us
  matrix products: 5.75 us -> 0 us
  local copies, waits for them, and re-layouts: 8.15 us -> 2.77 us
  other arithmetic: 3.65 us -> 0 us
    psum x2 -> x0, blocking collectives: 74.4 us -> none  [both_sums(): lax.psum((jnp.sum(residual * precond * inv_mult), jnp.sum(precond * appli...]
    ppermute x24 -> x0, waiting for transfers between devices: 44.1 us -> none  [the longest x12 31.7 us: padded(): before = lax.ppermute(last, axis, up)]
    pallas_call x0 -> x1, Pallas kernels: none -> 35 us  [local(): pl.pallas_call(functools.partial(kernel, ndom, nsub, local_barrier), out_...]
    ppermute x24 -> x0, starting transfers between devices: 21.7 us -> none  [the longest x12 11 us: padded(): before = lax.ppermute(last, axis, up)]
    dot_general x30 -> x0, matrix products: 5.75 us -> none  [the longest x10 2.46 us: derive(): jnp.einsum('bpqai,ji->bpqaj', blocks, block_matrix, precision=highest)]
    unnamed x27 -> x7, local copies, waits for them, and re-layouts: 6.38 us -> 2.77 us
    slice x24 -> x0, local copies, waits for them, and re-layouts: 1.78 us -> none  [the longest x1 0.81 us: local(): velocity[2:3] * gradients[2]]
  transfers between devices with their start and end apart: 24 -> 0, of which waited for: 24 -> 0; matrix products, arithmetic and copies ran while one was open for 1% -> 0% of each run, Pallas kernels for 0% -> 0%
where the time goes in v1:
time: 38.7 us; the launch traced here: 38.4 us
  Pallas kernels  35 us (90%)
  local copies, waits for them, and re-layouts  2.77 us (7%)
  between operations  0.65 us (2%)
    pallas_call x1, Pallas kernels, local(): pl.pallas_call(functools.partial(kernel, ndom, nsub, local_barrier), out_...  35 us
    unnamed x7, local copies, waits for them, and re-layouts  2.77 us

profile of v1, /device:TPU:0, one launch (start us, length us, event | category | flops | bytes accessed | tf_op | source)
XLA Modules:
  0.0 38.4 jit_solution(843660027486404859)
XLA Ops:
  0.6 35.0 %shard_map.76 = (f32[8,8,128]{2,1,0:T(8,128)}, f32[8,8,128]{2,1,0:T(8,128)}, f32[8,8,128]{2,1,0:T(8,128)}) custom-call(f32[8,8,128]{2,1,0:T(8,128)} %level_ref.1, f32[3,8,8,128]{3,2,1,0:T(8,128)} %velocity_ref.1, f32[8,8,128]{2,1,0:T(8,128)} %source_ref.1, f32[26,8,128]{2,1,0:T(8,128)} %constant.4.clone.planes_ref, bf16[3,128,256]{2,1,0:T(8,128)(2,1)} %constant.5.clone.wide_ref), custom_call_target="tpu_custom_call" | custom-call | tf_op jit(solution)/shard_map/pallas_call | solution.py:380
  35.6 0.0 copy-start.1
  35.6 1.4 %copy.11 = f32[8,8,128]{2,1,0:T(8,128)} copy(f32[8,8,128]{2,1,0:T(8,128)} %get-tuple-element.6) | data formatting | bytes 65536
  37.0 0.0 copy-done.1
  37.0 0.0 copy-start
  37.0 0.6 %copy.12 = f32[8,8,128]{2,1,0:T(8,128)} copy(f32[8,8,128]{2,1,0:T(8,128)S(1)} %copy-done.1) | data formatting | bytes 65536
  37.6 0.2 copy-done
  37.8 0.6 %copy.13 = f32[8,8,128]{2,1,0:T(8,128)} copy(f32[8,8,128]{2,1,0:T(8,128)S(1)} %copy-done) | data formatting | bytes 65536
Async XLA Ops:
  35.6 1.4 %copy-start.1 = (f32[8,8,128]{2,1,0:T(8,128)S(1)}, f32[8,8,128]{2,1,0:T(8,128)}, u32[]{:S(2)}) copy-start(f32[8,8,128]{2,1,0:T(8,128)} %get-tuple-element.7) | copy-start | bytes 98308
  37.0 0.8 %copy-start = (f32[8,8,128]{2,1,0:T(8,128)S(1)}, f32[8,8,128]{2,1,0:T(8,128)}, u32[]{:S(2)}) copy-start(f32[8,8,128]{2,1,0:T(8,128)} %get-tuple-element.8) | copy-start | bytes 98308

commit v2 on v1

--- a/solution.py
+++ b/solution.py
@@ -100,7 +100,7 @@
 
 def kernel(ndom, nsub, local_barrier, level_ref, velocity_ref, source_ref, planes_ref, wide_ref,
            new_ref, pressure_ref, correction_ref, *scratch):
-    (level_v, velocity_v, source_v, planes_v, wide_v, out_v, in_sem, out_sem,
+    (level_v, velocity_v, source_v, planes_v, wide_v, in_sem,
      face_send, face_recv, edge_send, edge_recv, sum_send, sum_recv,
      first_faces, first_edges, first_faces_in, first_edges_in,
      faces, edges, faces_in, edges_in, sums, sums_in) = scratch
@@ -292,25 +292,23 @@
         phi = [phi[i] + reinit_step * change[i] * inv_mult[i] for i in span]
 
     for i in span:
-        out_v[0, i] = phi[i]
-    stores = [pltpu.make_async_copy(out_v.at[n], ref, out_sem.at[n])
-              for n, ref in enumerate((new_ref, pressure_ref, correction_ref))]
-    stores[0].start()
+        new_ref[i] = phi[i]
     weighted = [weight[i] * (1.0 / (1.0 + density_ratio * phi[i] * phi[i])) for i in span]
     squares = divergence([weighted] * 3, SQUARE)
     diagonal = assemble(step, [weight[i] + squares[i] for i in span])
     step += 1
     inverse = [1.0 / v for v in diagonal]
 
-    def operate(values):
-        parts = [[weighted[i] * g[i] for i in span] for g in gradient(values)]
+    def apply(step, sum_step, residual, precond):
+        slopes = gradient(precond)
+        parts = [[weighted[i] * g[i] for i in span] for g in slopes]
+        mass = [weight[i] * precond[i] for i in span]
+        energy = dot(precond, mass)
+        for slope, part in zip(slopes, parts):
+            energy = energy + dot(slope, part)
+        begin_sums(sum_step, dot(residual, precond, inv_mult), energy)
         total = divergence(parts, TRANS)
-        return [weight[i] * values[i] + total[i] for i in span]
-
-    def apply(step, sum_step, residual, precond):
-        partial = operate(precond)
-        sent = begin(step, partial)
-        begin_sums(sum_step, dot(residual, precond, inv_mult), dot(precond, partial))
+        sent = begin(step, [mass[i] + total[i] for i in span])
         applied = finish(step, sent)
         return (applied,) + finish_sums(sum_step)
 
@@ -335,10 +333,8 @@
             image = [applied[i] + ratio * image[i] for i in span]
             norm_now = norm_next
     for i in span:
-        out_v[1, i] = result[i]
-        out_v[2, i] = residual[i] * inverse[i]
-    stores[1].start()
-    stores[2].start()
+        pressure_ref[i] = result[i]
+        correction_ref[i] = residual[i] * inverse[i]
     pltpu.make_async_copy(first_faces, first_faces, face_send.at[0]).wait()
     pltpu.make_async_copy(first_edges, first_edges, edge_send.at[0]).wait()
     for s in range(step):
@@ -346,8 +342,15 @@
         pltpu.make_async_copy(edges.at[s], edges.at[s], edge_send.at[s + 1]).wait()
     for s in range(PITERS):
         pltpu.make_async_copy(sums_in.at[s], sums_in.at[s], sum_send.at[s]).wait()
-    for store in stores:
-        store.wait()
+
+
+def write_out(a_in, b_in, c_in, a_out, b_out, c_out, sem):
+    copies = [pltpu.make_async_copy(src, dst, sem.at[i]) for i, (src, dst) in enumerate((
+        (a_in, a_out), (b_in, b_out), (c_in, c_out)))]
+    for copy in copies:
+        copy.start()
+    for copy in copies:
+        copy.wait()
 
 
 def solution(mesh):
@@ -366,7 +369,7 @@
         scratch = [
             vmem(level_set.shape), vmem(velocity.shape), vmem(source.shape),
             vmem(planes.shape), pltpu.VMEM(wide.shape, jnp.bfloat16),
-            vmem((3,) + level_set.shape), dma((5,)), dma((3,)),
+            dma((5,)),
             dma((rounds + 1,)), dma((rounds + 1,)), dma((rounds + 1,)), dma((rounds + 1,)),
             dma((PITERS,)), dma((PITERS,)),
             vmem((4, 2) + tile), vmem((4, 2, 1, lanes)),
@@ -376,15 +379,26 @@
             vmem((PITERS, 2, lanes)), vmem((PITERS, others, 2, lanes)),
         ]
         any_space = pl.BlockSpec(memory_space=pl.ANY)
+        hbm_space = pl.BlockSpec(memory_space=pltpu.HBM)
         out = jax.ShapeDtypeStruct(level_set.shape, jnp.float32)
+        held = pltpu.VMEM(level_set.shape, jnp.float32)
+        results = pl.pallas_call(
+            functools.partial(kernel, ndom, nsub, local_barrier),
+            out_shape=(held, held, held),
+            in_specs=[hbm_space] * 5,
+            out_specs=(pl.BlockSpec(memory_space=pltpu.VMEM),) * 3,
+            scratch_shapes=scratch,
+            compiler_params=pltpu.CompilerParams(
+                collective_id=0, has_side_effects=True, vmem_limit_bytes=60 * 2**20),
+        )(level_set, velocity, source, jnp.asarray(planes), jnp.asarray(wide))
         return pl.pallas_call(
-            functools.partial(kernel, ndom, nsub, local_barrier),
+            write_out,
             out_shape=(out, out, out),
-            in_specs=[any_space] * 5,
-            out_specs=(any_space,) * 3,
-            scratch_shapes=scratch,
-            compiler_params=pltpu.CompilerParams(collective_id=0, has_side_effects=True),
-        )(level_set, velocity, source, jnp.asarray(planes), jnp.asarray(wide))
+            in_specs=[any_space] * 3,
+            out_specs=(hbm_space,) * 3,
+            scratch_shapes=[dma((3,))],
+            compiler_params=pltpu.CompilerParams(vmem_limit_bytes=2**20),
+        )(*results)
 
     return jax.shard_map(
         local,

time: 38.7 us -> 35.4 us (0.915)
  local copies, waits for them, and re-layouts: 2.77 us -> 0 us
  Pallas kernels: 35 us -> 34.6 us
    unnamed x7 -> x0, local copies, waits for them, and re-layouts: 2.77 us -> none
    pallas_call x1, Pallas kernels: 35 us -> 33.9 us  [local(): pl.pallas_call(functools.partial(kernel, ndom, nsub, local_barrier), out_...]
    pallas_call x0 -> x1, Pallas kernels: none -> 0.67 us  [local(): pl.pallas_call(write_out, out_shape=(out, out, out), in_specs=[any_space]...]
where the time goes in v2:
time: 35.4 us; the launch traced here: 35.2 us
  Pallas kernels  34.6 us (98%)
  between operations  0.64 us (2%)
    pallas_call x1, Pallas kernels, local(): pl.pallas_call(functools.partial(kernel, ndom, nsub, local_barrier), out_...  33.9 us

profile of v2, /device:TPU:0, one launch (start us, length us, event | category | flops | bytes accessed | tf_op | source)
XLA Modules:
  0.0 35.2 jit_solution(15879861489996175632)
XLA Ops:
  0.6 33.9 %shard_map.76 = (f32[8,8,128]{2,1,0:T(8,128)S(1)}, f32[8,8,128]{2,1,0:T(8,128)S(1)}, f32[8,8,128]{2,1,0:T(8,128)S(1)}) custom-call(f32[8,8,128]{2,1,0:T(8,128)} %level_ref.1, f32[3,8,8,128]{3,2,1,0:T(8,128)} %velocity_ref.1, f32[8,8,128]{2,1,0:T(8,128)} %source_ref.1, f32[26,8,128]{2,1,0:T(8,128)} %constant.4.clone.planes_ref, ...), custom_call_target="tpu_custom_call" | custom-call | tf_op jit(solution)/shard_map/pallas_call | solution.py:385
  34.6 0.7 %shard_map.77 = (f32[8,8,128]{2,1,0:T(8,128)}, f32[8,8,128]{2,1,0:T(8,128)}, f32[8,8,128]{2,1,0:T(8,128)}) custom-call(f32[8,8,128]{2,1,0:T(8,128)S(1)} %get-tuple-element.6.a_in, f32[8,8,128]{2,1,0:T(8,128)S(1)} %get-tuple-element.7.b_in, f32[8,8,128]{2,1,0:T(8,128)S(1)} %get-tuple-element.8.c_in), custom_call_target="tpu_custom_call" | custom-call | tf_op jit(solution)/shard_map/pallas_call | solution.py:394

commit v3 on v2

--- a/solution.py
+++ b/solution.py
@@ -102,7 +102,6 @@
            new_ref, pressure_ref, correction_ref, *scratch):
     (level_v, velocity_v, source_v, planes_v, wide_v, in_sem,
      face_send, face_recv, edge_send, edge_recv, sum_send, sum_recv,
-     first_faces, first_edges, first_faces_in, first_edges_in,
      faces, edges, faces_in, edges_in, sums, sums_in) = scratch
     dom, sub = lax.axis_index("dom"), lax.axis_index("sub")
 
@@ -169,60 +168,47 @@
         first, second = along_first(parts[0], kind), along_second(parts[1], kind)
         return [(first[i] + second[i]) + third[i] for i in span]
 
-    def send(slot, fields, face_out, edge_out, face_in, edge_in):
-        fields = [[fold_lanes(v) for v in field] for field in fields]
-        for n, field in enumerate(fields):
-            face_out[0, n] = field[ORDER - 1]
-            face_out[1, n] = field[0]
-            right = jnp.concatenate([v[ORDER - 1:] for v in field], axis=0)
-            left = jnp.concatenate([v[:1] for v in field], axis=0)
-            face_out[2, n] = right
-            face_out[3, n] = left
-            edge_out[0, n] = field[ORDER - 1][ORDER - 1:]
-            edge_out[1, n] = field[ORDER - 1][:1]
-            edge_out[2, n] = field[0][ORDER - 1:]
-            edge_out[3, n] = field[0][:1]
+    def begin(step, field):
+        face_out, edge_out = faces.at[step], edges.at[step]
+        last, first = fold_lanes(field[ORDER - 1]), fold_lanes(field[0])
+        face_out[0], face_out[1] = last, first
+        edge_out[0], edge_out[1] = last[ORDER - 1:], last[:1]
+        edge_out[2], edge_out[3] = first[ORDER - 1:], first[:1]
+
+        def post_face(i, a, b):
+            pltpu.make_async_remote_copy(
+                face_out.at[i], faces_in.at[step, i], face_send.at[step], face_recv.at[step],
+                device_id=peer(a, b), device_id_type=MESH).start()
+
         for i, (a, b) in enumerate(((1, 1), (1, -1), (-1, 1), (-1, -1))):
             pltpu.make_async_remote_copy(
-                edge_out.at[i], edge_in.at[i], edge_send.at[slot], edge_recv.at[slot],
+                edge_out.at[i], edges_in.at[step, i], edge_send.at[step], edge_recv.at[step],
                 device_id=peer(a, b), device_id_type=MESH).start()
-        for i, (a, b) in enumerate(((1, 0), (-1, 0), (0, 1), (0, -1))):
-            pltpu.make_async_remote_copy(
-                face_out.at[i], face_in.at[i], face_send.at[slot], face_recv.at[slot],
-                device_id=peer(a, b), device_id_type=MESH).start()
-        return fields
-
-    def receive(slot, fields, face_in, edge_in):
-        pltpu.make_async_copy(face_in, face_in, face_recv.at[slot]).wait()
-        pltpu.make_async_copy(edge_in, edge_in, edge_recv.at[slot]).wait()
-        results = []
-        for n, field in enumerate(fields):
-            result = list(field)
-            result[0] = result[0] + face_in[0, n]
-            result[ORDER - 1] = result[ORDER - 1] + face_in[1, n]
-            for i, (at, mask_a, mask_b) in enumerate((
-                    (0, row_first, row_last), (ORDER - 1, row_first, row_last))):
-                result[at] = result[at] + jnp.where(
-                    mask_a, edge_in[2 * i, n],
-                    jnp.where(mask_b, edge_in[2 * i + 1, n], 0.0))
-            for i in span:
-                result[i] = result[i] + jnp.where(
-                    row_first, face_in[2, n, i:i + 1],
-                    jnp.where(row_last, face_in[3, n, i:i + 1], 0.0))
-            results.append(result)
-        return results
-
-    def begin(step, field):
-        buffers = (faces.at[step], edges.at[step], faces_in.at[step], edges_in.at[step])
-        return send(step + 1, [field], *buffers)
+        post_face(0, 1, 0)
+        post_face(1, -1, 0)
+        face_out[2] = fold_lanes(jnp.concatenate([v[ORDER - 1:] for v in field], axis=0))
+        face_out[3] = fold_lanes(jnp.concatenate([v[:1] for v in field], axis=0))
+        post_face(2, 0, 1)
+        post_face(3, 0, -1)
+        return [first] + [fold_lanes(v) for v in field[1:-1]] + [last]
 
     def finish(step, field):
-        return receive(step + 1, field, faces_in.at[step], edges_in.at[step])[0]
+        face_in, edge_in = faces_in.at[step], edges_in.at[step]
+        pltpu.make_async_copy(face_in, face_in, face_recv.at[step]).wait()
+        pltpu.make_async_copy(edge_in, edge_in, edge_recv.at[step]).wait()
+        result = list(field)
+        for i, at in enumerate((0, ORDER - 1)):
+            result[at] = result[at] + face_in[i] + jnp.where(
+                row_first, edge_in[2 * i], jnp.where(row_last, edge_in[2 * i + 1], 0.0))
+        for i in span:
+            result[i] = result[i] + jnp.where(
+                row_first, face_in[2, i:i + 1], jnp.where(row_last, face_in[3, i:i + 1], 0.0))
+        return result
 
     def assemble(step, field):
         return finish(step, begin(step, field))
 
-    hops = sorted(range(ndom), key=lambda a: -min(a, ndom - a))
+    hops = sorted(range(ndom), key=lambda a: min(a, ndom - a) or ndom)
     others = [(a, b) for a in hops for b in (2, 1, 3, 0) if a or b] if nsub == 4 else [
         (a, b) for a in hops for b in range(nsub) if a or b]
 
@@ -270,14 +256,14 @@
     advected = [
         phi[i] - advect_step * (velocity_v[0, i] * g0[i] + velocity_v[1, i] * g1[i]
                                 + velocity_v[2, i] * g2[i]) for i in span]
+    pl.semaphore_wait(barrier, len(near) if local_barrier else ndom * nsub - 1)
+    sent = begin(0, advected)
     loads[4].wait()
-    right = [weight[i] * source_v[i] for i in span]
-    pl.semaphore_wait(barrier, len(near) if local_barrier else ndom * nsub - 1)
-    fields = send(0, [advected, right], first_faces, first_edges, first_faces_in, first_edges_in)
-    phi, right = receive(0, fields, first_faces_in, first_edges_in)
+    sent_right = begin(1, [weight[i] * source_v[i] for i in span])
+    phi = finish(0, sent)
     phi = [phi[i] * inv_mult[i] for i in span]
 
-    step = 0
+    step = 2
     for sweep in range(SWEEPS):
         g0, g1, g2 = gradient(phi)
         if sweep == 0:
@@ -312,7 +298,7 @@
         applied = finish(step, sent)
         return (applied,) + finish_sums(sum_step)
 
-    residual = right
+    residual = finish(1, sent_right)
     precond = [residual[i] * inverse[i] for i in span]
     applied, norm_now, product = apply(step, 0, residual, precond)
     step += 1
@@ -335,11 +321,9 @@
     for i in span:
         pressure_ref[i] = result[i]
         correction_ref[i] = residual[i] * inverse[i]
-    pltpu.make_async_copy(first_faces, first_faces, face_send.at[0]).wait()
-    pltpu.make_async_copy(first_edges, first_edges, edge_send.at[0]).wait()
     for s in range(step):
-        pltpu.make_async_copy(faces.at[s], faces.at[s], face_send.at[s + 1]).wait()
-        pltpu.make_async_copy(edges.at[s], edges.at[s], edge_send.at[s + 1]).wait()
+        pltpu.make_async_copy(faces.at[s], faces.at[s], face_send.at[s]).wait()
+        pltpu.make_async_copy(edges.at[s], edges.at[s], edge_send.at[s]).wait()
     for s in range(PITERS):
         pltpu.make_async_copy(sums_in.at[s], sums_in.at[s], sum_send.at[s]).wait()
 
@@ -355,7 +339,7 @@
 
 def solution(mesh):
     ndom, nsub = mesh.shape["dom"], mesh.shape["sub"]
-    rounds = SWEEPS + 1 + PITERS
+    rounds = SWEEPS + 3 + PITERS
     local_barrier = max(ndom, nsub) // 2 <= SWEEPS + 3
 
     def local(level_set, velocity, source):
@@ -370,12 +354,10 @@
             vmem(level_set.shape), vmem(velocity.shape), vmem(source.shape),
             vmem(planes.shape), pltpu.VMEM(wide.shape, jnp.bfloat16),
             dma((5,)),
-            dma((rounds + 1,)), dma((rounds + 1,)), dma((rounds + 1,)), dma((rounds + 1,)),
+            dma((rounds,)), dma((rounds,)), dma((rounds,)), dma((rounds,)),
             dma((PITERS,)), dma((PITERS,)),
-            vmem((4, 2) + tile), vmem((4, 2, 1, lanes)),
-            vmem((4, 2) + tile), vmem((4, 2, 1, lanes)),
-            vmem((rounds, 4, 1) + tile), vmem((rounds, 4, 1, 1, lanes)),
-            vmem((rounds, 4, 1) + tile), vmem((rounds, 4, 1, 1, lanes)),
+            vmem((rounds, 4) + tile), vmem((rounds, 4, 1, lanes)),
+            vmem((rounds, 4) + tile), vmem((rounds, 4, 1, lanes)),
             vmem((PITERS, 2, lanes)), vmem((PITERS, others, 2, lanes)),
         ]
         any_space = pl.BlockSpec(memory_space=pl.ANY)

time: 35.4 us -> 35.1 us (level)
  no operation moved by 1% of the time
where the time goes in v3:
time: 35.1 us; the launch traced here: 34.9 us
  Pallas kernels  34.3 us (98%)
  between operations  0.64 us (2%)
    pallas_call x1, Pallas kernels, local(): pl.pallas_call(functools.partial(kernel, ndom, nsub, local_barrier), out_...  33.6 us

profile of v3, /device:TPU:0, one launch (start us, length us, event | category | flops | bytes accessed | tf_op | source)
XLA Modules:
  0.0 34.9 jit_solution(2638580786813023003)
XLA Ops:
  0.6 33.6 %shard_map.76 = (f32[8,8,128]{2,1,0:T(8,128)S(1)}, f32[8,8,128]{2,1,0:T(8,128)S(1)}, f32[8,8,128]{2,1,0:T(8,128)S(1)}) custom-call(f32[8,8,128]{2,1,0:T(8,128)} %level_ref.1, f32[3,8,8,128]{3,2,1,0:T(8,128)} %velocity_ref.1, f32[8,8,128]{2,1,0:T(8,128)} %source_ref.1, f32[26,8,128]{2,1,0:T(8,128)} %constant.4.clone.planes_ref, ...), custom_call_target="tpu_custom_call" | custom-call | tf_op jit(solution)/shard_map/pallas_call | solution.py:367
  34.3 0.7 %shard_map.77 = (f32[8,8,128]{2,1,0:T(8,128)}, f32[8,8,128]{2,1,0:T(8,128)}, f32[8,8,128]{2,1,0:T(8,128)}) custom-call(f32[8,8,128]{2,1,0:T(8,128)S(1)} %get-tuple-element.6.a_in, f32[8,8,128]{2,1,0:T(8,128)S(1)} %get-tuple-element.7.b_in, f32[8,8,128]{2,1,0:T(8,128)S(1)} %get-tuple-element.8.c_in), custom_call_target="tpu_custom_call" | custom-call | tf_op jit(solution)/shard_map/pallas_call | solution.py:376

commit v4 on v3

--- a/solution.py
+++ b/solution.py
@@ -168,6 +168,10 @@
         first, second = along_first(parts[0], kind), along_second(parts[1], kind)
         return [(first[i] + second[i]) + third[i] for i in span]
 
+    upper = dom // (ndom // 2)
+    ways = ((1 - upper, lax.rem(dom + 2 * upper - 1 + ndom, ndom)),
+            (upper, lax.rem(dom - 2 * upper + 1 + ndom, ndom)))
+
     def begin(step, field):
         face_out, edge_out = faces.at[step], edges.at[step]
         last, first = fold_lanes(field[ORDER - 1]), fold_lanes(field[0])
@@ -175,21 +179,20 @@
         edge_out[0], edge_out[1] = last[ORDER - 1:], last[:1]
         edge_out[2], edge_out[3] = first[ORDER - 1:], first[:1]
 
-        def post_face(i, a, b):
+        def post(out, into, slot, sends, receives, target):
             pltpu.make_async_remote_copy(
-                face_out.at[i], faces_in.at[step, i], face_send.at[step], face_recv.at[step],
-                device_id=peer(a, b), device_id_type=MESH).start()
-
-        for i, (a, b) in enumerate(((1, 1), (1, -1), (-1, 1), (-1, -1))):
-            pltpu.make_async_remote_copy(
-                edge_out.at[i], edges_in.at[step, i], edge_send.at[step], edge_recv.at[step],
-                device_id=peer(a, b), device_id_type=MESH).start()
-        post_face(0, 1, 0)
-        post_face(1, -1, 0)
+                out.at[slot], into.at[step, slot], sends.at[step], receives.at[step],
+                device_id=target, device_id_type=MESH).start()
+
+        for slot, beside in ways:
+            for j, b in enumerate((1, -1)):
+                post(edge_out, edges_in, 2 * slot + j, edge_send, edge_recv,
+                     (beside, lax.rem(sub + b % nsub, nsub)))
+            post(face_out, faces_in, slot, face_send, face_recv, (beside, sub))
         face_out[2] = fold_lanes(jnp.concatenate([v[ORDER - 1:] for v in field], axis=0))
         face_out[3] = fold_lanes(jnp.concatenate([v[:1] for v in field], axis=0))
-        post_face(2, 0, 1)
-        post_face(3, 0, -1)
+        post(face_out, faces_in, 2, face_send, face_recv, peer(0, 1))
+        post(face_out, faces_in, 3, face_send, face_recv, peer(0, -1))
         return [first] + [fold_lanes(v) for v in field[1:-1]] + [last]
 
     def finish(step, field):

time: 35.1 us -> 35 us (level)
  no operation moved by 1% of the time
where the time goes in v4:
time: 35 us; the launch traced here: 34.9 us
  Pallas kernels  34.3 us (98%)
  between operations  0.64 us (2%)
    pallas_call x1, Pallas kernels, local(): pl.pallas_call(functools.partial(kernel, ndom, nsub, local_barrier), out_...  33.6 us

profile of v4, /device:TPU:0, one launch (start us, length us, event | category | flops | bytes accessed | tf_op | source)
XLA Modules:
  0.0 34.9 jit_solution(17011066250049872296)
XLA Ops:
  0.6 33.6 %shard_map.76 = (f32[8,8,128]{2,1,0:T(8,128)S(1)}, f32[8,8,128]{2,1,0:T(8,128)S(1)}, f32[8,8,128]{2,1,0:T(8,128)S(1)}) custom-call(f32[8,8,128]{2,1,0:T(8,128)} %level_ref.1, f32[3,8,8,128]{3,2,1,0:T(8,128)} %velocity_ref.1, f32[8,8,128]{2,1,0:T(8,128)} %source_ref.1, f32[26,8,128]{2,1,0:T(8,128)} %constant.4.clone.planes_ref, ...), custom_call_target="tpu_custom_call" | custom-call | tf_op jit(solution)/shard_map/pallas_call | solution.py:370
  34.2 0.7 %shard_map.77 = (f32[8,8,128]{2,1,0:T(8,128)}, f32[8,8,128]{2,1,0:T(8,128)}, f32[8,8,128]{2,1,0:T(8,128)}) custom-call(f32[8,8,128]{2,1,0:T(8,128)S(1)} %get-tuple-element.6.a_in, f32[8,8,128]{2,1,0:T(8,128)S(1)} %get-tuple-element.7.b_in, f32[8,8,128]{2,1,0:T(8,128)S(1)} %get-tuple-element.8.c_in), custom_call_target="tpu_custom_call" | custom-call | tf_op jit(solution)/shard_map/pallas_call | solution.py:379

commit v5 on v4

--- a/solution.py
+++ b/solution.py
@@ -219,14 +219,18 @@
         sums[step, 0:1] = jnp.sum(first, axis=0, keepdims=True)
         sums[step, 1:2] = jnp.sum(second, axis=0, keepdims=True)
 
+        post_sums(step, True)
+
+    def post_sums(step, far):
         def post(target, k):
             pltpu.make_async_remote_copy(
                 sums.at[step], sums_in.at[step, k], sum_send.at[step], sum_recv.at[step],
                 device_id=target, device_id_type=MESH).start()
         if ndom * nsub <= 64:
             for k, (a, b) in enumerate(others):
-                post(peer(a, b), k)
-        else:
+                if (k < len(others) // 2) == far:
+                    post(peer(a, b), k)
+        elif far:
             @pl.loop(1, ndom * nsub)
             def _(k):
                 post((lax.rem(dom + k // nsub, ndom), lax.rem(sub + k % nsub, nsub)), k - 1)
@@ -298,6 +302,7 @@
         begin_sums(sum_step, dot(residual, precond, inv_mult), energy)
         total = divergence(parts, TRANS)
         sent = begin(step, [mass[i] + total[i] for i in span])
+        post_sums(sum_step, False)
         applied = finish(step, sent)
         return (applied,) + finish_sums(sum_step)
 

time: 35 us -> 34.9 us (level)
  no operation moved by 1% of the time
where the time goes in v5:
time: 34.9 us; the launch traced here: 34.8 us
  Pallas kernels  34.1 us (98%)
  between operations  0.64 us (2%)
    pallas_call x1, Pallas kernels, local(): pl.pallas_call(functools.partial(kernel, ndom, nsub, local_barrier), out_...  33.5 us

profile of v5, /device:TPU:0, one launch (start us, length us, event | category | flops | bytes accessed | tf_op | source)
XLA Modules:
  0.0 34.8 jit_solution(13063249911047968532)
XLA Ops:
  0.6 33.5 %shard_map.76 = (f32[8,8,128]{2,1,0:T(8,128)S(1)}, f32[8,8,128]{2,1,0:T(8,128)S(1)}, f32[8,8,128]{2,1,0:T(8,128)S(1)}) custom-call(f32[8,8,128]{2,1,0:T(8,128)} %level_ref.1, f32[3,8,8,128]{3,2,1,0:T(8,128)} %velocity_ref.1, f32[8,8,128]{2,1,0:T(8,128)} %source_ref.1, f32[26,8,128]{2,1,0:T(8,128)} %constant.4.clone.planes_ref, ...), custom_call_target="tpu_custom_call" | custom-call | tf_op jit(solution)/shard_map/pallas_call | solution.py:375
  34.1 0.7 %shard_map.77 = (f32[8,8,128]{2,1,0:T(8,128)}, f32[8,8,128]{2,1,0:T(8,128)}, f32[8,8,128]{2,1,0:T(8,128)}) custom-call(f32[8,8,128]{2,1,0:T(8,128)S(1)} %get-tuple-element.6.a_in, f32[8,8,128]{2,1,0:T(8,128)S(1)} %get-tuple-element.7.b_in, f32[8,8,128]{2,1,0:T(8,128)S(1)} %get-tuple-element.8.c_in), custom_call_target="tpu_custom_call" | custom-call | tf_op jit(solution)/shard_map/pallas_call | solution.py:384
